TPU v7x, 32 devices: a whole 2x2x4 slice. The times are simulated.
32 devices in a mesh: term: 8 (over z, core), sector: 4 (over y, x).
Axes of the slice: x: 2, y: 2, z: 4, core: 2. Of those that a mesh axis runs over, the one named last changes fastest.
Arguments:
- wavefunction: bfloat16 [24, 256, 256], P('sector'), may hold values from -6 to 6
- left_env: bfloat16 [24, 24, 256, 256], P('term', 'sector')
- right_env: bfloat16 [24, 24, 256, 256], P('term', 'sector')
- source: int32 [24, 24], P('term'), may hold values from 0 to 23, as said below
- block_size: int32 [24, 2], P('sector'), may hold values from 32 to 256
Outputs:
- first_product: float32 [24, 256, 256], P('sector', 'term')
- second_product: float32 [24, 256, 256], P('sector', 'term')
Inputs may be any that keep to these rules, and one draw needn't show every extreme that they name: Owner of sector s is s // 6. Among the 3 x 6 entries of source in one device's rows (one index of term) and columns (one index of sector), at most 5 name sectors of any one owner, and some owner is named exactly 5 times.
All inputs are finite; a program needn't handle non-finite values.
Results may differ from a plain program's by a relative error of at most 0.0037.
Values may be sent and summed in bfloat16 or wider, within the bound.
A program may use at most 64 MiB of HBM per device.

v0:
```python
import jax
import jax.numpy as jnp
from jax import lax
from jax.sharding import PartitionSpec as P

epsilon = 1e-06


def block_mask(block_size, width):
    positions = jnp.arange(width, dtype=jnp.int32)
    row_keep = positions[None, :] < block_size[:, 0:1]
    column_keep = positions[None, :] < block_size[:, 1:2]
    return row_keep[:, :, None] & column_keep[:, None, :]


def fetch_blocks(masked, source):
    local_count = masked.shape[0]
    width = masked.shape[1]
    bond_count = source.shape[0]
    my_index = lax.axis_index("sector")
    item_count = bond_count * local_count
    wanted = lax.dynamic_slice_in_dim(source, my_index * local_count, local_count, 1).reshape(
        item_count
    )
    pieces = lax.all_gather(masked, "sector", axis=0, tiled=True)
    piece_count = pieces.shape[0]
    numbers = jnp.arange(piece_count, dtype=jnp.int32)
    onehot = (wanted[:, None] == numbers[None, :]).astype(jnp.bfloat16)
    picked = jnp.dot(
        onehot, pieces.reshape(piece_count, width * width), preferred_element_type=jnp.float32
    )
    return picked.astype(jnp.bfloat16).reshape(bond_count, local_count, width, width)


def apply_operator(vector, left_env, right_env, source, keep):
    masked = jnp.where(keep, vector, jnp.zeros_like(vector))
    picked = fetch_blocks(masked, source)
    half_product = jnp.einsum(
        "bkij,bkjl->bkil", left_env, picked, preferred_element_type=jnp.float32
    ).astype(jnp.bfloat16)
    bond_terms = jnp.einsum(
        "bkil,bkml->bkim", half_product, right_env, preferred_element_type=jnp.float32
    )
    summed = jnp.sum(bond_terms, axis=0)
    return (jnp.where(keep, summed, jnp.zeros_like(summed)), masked)


def body(wavefunction, left_env, right_env, source, block_size):
    width = wavefunction.shape[1]
    keep = block_mask(block_size, width)
    term_count = lax.axis_size("term")
    term_index = lax.axis_index("term")
    row_count = width // term_count
    total_count = lax.axis_size("sector") * wavefunction.shape[0] * width * width
    partial_value, masked = apply_operator(wavefunction, left_env, right_env, source, keep)
    masked_float = masked.astype(jnp.float32)
    whole_sum = lax.psum(partial_value, "term")
    first_product = lax.dynamic_slice_in_dim(whole_sum, term_index * row_count, row_count, 1)
    margin, self_norm = lax.psum(
        (jnp.sum(masked_float * whole_sum), jnp.sum(masked_float * masked_float)), "sector"
    )
    residual = whole_sum - margin / self_norm * masked_float
    spread = lax.psum(jnp.sum(residual * residual), "sector")
    next_vector = (residual * lax.rsqrt(spread / total_count + epsilon)).astype(jnp.bfloat16)
    second_partial, _ = apply_operator(next_vector, left_env, right_env, source, keep)
    second_product = lax.psum_scatter(second_partial, "term", scatter_dimension=1, tiled=True)
    return (first_product, second_product)


def solution(mesh):
    placed = (
        P("sector", None, None),
        P("term", "sector", None, None),
        P("term", "sector", None, None),
        P("term", None),
        P("sector", None),
    )
    return jax.shard_map(
        body,
        mesh=mesh,
        in_specs=placed,
        out_specs=(P("sector", "term", None), P("sector", "term", None)),
        check_vma=False,
    )
```

profile of v0, /device:TPU:0, one launch (start us, length us, event | category | flops | bytes accessed | tf_op | source)
XLA Modules:
  0.0 256.0 jit_solution(13237176541998194756)
XLA Ops:
  7.2 0.0 copy-start
  7.2 0.0 copy-start.2
  7.2 0.0 all-gather.3.cloned.1.call-start
  7.2 0.9 slice_bitcast_fusion.1
  8.1 0.1 iota_compare_fusion.3
  8.2 2.3 and_select_fusion.3
  10.5 0.0 all-gather.3.cloned.1.call-update
  10.5 0.0 all-reduce.3.cloned.1.call-start
  10.6 0.0 copy-done.2
  10.6 0.1 constant_dynamic-slice_fusion.1
  10.7 0.1 eq.8
  10.8 46.5 %all-gather.3.cloned.1.call-done = bf16[24,256,256]{2,1,0:T(8,128)(2,1)} async-done(((bf16[6,256,256]{2,1,0:T(8,128)(2,1)}), bf16[24,256,256]{2,1,0:T(8,128)(2,1)}) %all-gather.3.cloned.1.call-update) | async-done | bytes 3145744 | tf_op jit(solution)/shard_map/all_gather | solution.py:25
  57.3 3.7 %copy.16 = bf16[3,8,256,256]{3,1,2,0:T(8,128)(2,1)S(1)} copy(bf16[3,8,256,256]{3,2,1,0:T(8,128)(2,1)} %bitcast.40) | data formatting | bytes 6291456
  60.9 1.0 convolution_convert_fusion.1
  62.0 0.7 copy.17
  62.7 1.7 slice.11
  64.4 0.0 copy-done
  64.4 0.0 copy-start.1
  64.4 5.0 %and_select_fusion.2 = f32[6,256,256]{2,1,0:T(8,128)} fusion(bf16[3,6,256,256]{3,2,1,0:T(8,128)(2,1)S(1)} %copy-done, bf16[3,6,256,256]{3,2,1,0:T(8,128)(2,1)} %bitcast.43, bf16[3,6,256,256]{3,2,1,0:T(8,128)(2,1)} %param.6, pred[6,256]{1,0:T(8,128)(4,1)S(1)} %get-tuple-element.8, pred[6,256]{1,0:T(8,128)(4,1)S(1)} %get-tuple-element.9), kind=kOutput, calls=%fused_computation.4 | convolution fusion | flops 1209925632 | bytes 8653824 | tf_op jit(solution)/shard_map/bkil,bkml->bkim/dot_general | solution.py:41
  69.4 0.0 all-reduce.3.cloned.1.call-update
  69.4 0.0 all-gather.5.cloned.1.call-start
  69.5 62.0 %all-reduce.3.cloned.1.call-done = f32[6,256,256]{2,1,0:T(8,128)} async-done(((f32[6,256,256]{2,1,0:T(8,128)}), f32[6,256,256]{2,1,0:T(8,128)}) %all-reduce.3.cloned.1.call-update) | async-done | bytes 1572880 | tf_op jit(solution)/shard_map/psum | solution.py:57
  131.5 0.0 copy-done.1
  131.5 2.6 %fusion.25 = (f32[]{:T(128)}, f32[]{:T(128)}) fusion(f32[6,256,256]{2,1,0:T(8,128)} %all-reduce.3.cloned.1.call-done, bf16[6,256,256]{2,1,0:T(8,128)(2,1)S(1)} %copy-done.1, pred[6,256]{1,0:T(8,128)(4,1)S(1)} %get-tuple-element.8, pred[6,256]{1,0:T(8,128)(4,1)S(1)} %get-tuple-element.9), kind=kLoop, calls=%fused_computation.24 | loop fusion | flops 2752510 | bytes 2362376 | tf_op jit(solution)/shard_map/reduce_sum | solution.py:60
  134.1 10.4 %all-reduce = (f32[]{:T(128)}, f32[]{:T(128)}) all-reduce(f32[]{:T(128)} %get-tuple-element.3, f32[]{:T(128)} %get-tuple-element.2), channel_id=1, replica_groups=mesh['term'=8,'sector'=4] {'sector'}, use_global_device_ids=true, to_apply=%region_2.3 | all-reduce | flops 2 | bytes 16 | tf_op jit(solution)/shard_map/psum | solution.py:59
  145.9 2.6 %multiply_reduce_fusion = f32[]{:T(128)} fusion(f32[6,256,256]{2,1,0:T(8,128)} %all-reduce.3.cloned.1.call-done, f32[]{:T(128)S(6)} %div.6, bf16[6,256,256]{2,1,0:T(8,128)(2,1)S(1)} %copy-done.1, pred[6,256]{1,0:T(8,128)(4,1)S(1)} %get-tuple-element.8, pred[6,256]{1,0:T(8,128)(4,1)S(1)} %get-tuple-element.9), kind=kLoop, calls=%fused_computation.27 | loop fusion | flops 2752511 | bytes 2362376 | tf_op jit(solution)/shard_map/reduce_sum | solution.py:63
  148.5 8.6 %psum.31 = f32[]{:T(128)} all-reduce(f32[]{:T(128)} %multiply_reduce_fusion), channel_id=1, replica_groups=mesh['term'=8,'sector'=4] {'sector'}, use_global_device_ids=true, to_apply=%region_6.7 | all-reduce | flops 1 | bytes 8 | tf_op jit(solution)/shard_map/psum | solution.py:63
  157.8 2.8 %and_select_fusion.1 = bf16[6,256,256]{2,1,0:T(8,128)(2,1)} fusion(f32[6,256,256]{2,1,0:T(8,128)} %all-reduce.3.cloned.1.call-done, f32[]{:T(128)S(6)} %rsqrt.3, f32[]{:T(128)S(6)} %div.6, pred[6,256]{1,0:T(8,128)(4,1)S(1)} %get-tuple-element.8, pred[6,256]{1,0:T(8,128)(4,1)S(1)} %get-tuple-element.9, bf16[6,256,256]{2,1,0:T(8,128)(2,1)S(1)} %copy-done.1), kind=kLoop, calls=%fused_computation.3 | loop fusion | flops 3145728 | bytes 3148808 | tf_op jit(solution)/shard_map/jit(_where)/select_n | solution.py:36
  160.6 0.0 all-gather.5.cloned.1.call-update
  160.6 0.2 reduce-scatter.2.cloned.1.call-start
  160.8 42.1 %all-gather.5.cloned.1.call-done = bf16[24,256,256]{2,1,0:T(8,128)(2,1)} async-done(((bf16[6,256,256]{2,1,0:T(8,128)(2,1)}), bf16[24,256,256]{2,1,0:T(8,128)(2,1)}) %all-gather.5.cloned.1.call-update) | async-done | bytes 3145744 | tf_op jit(solution)/shard_map/all_gather | solution.py:25
  203.0 3.7 %copy.18 = bf16[3,8,256,256]{3,1,2,0:T(8,128)(2,1)S(1)} copy(bf16[3,8,256,256]{3,2,1,0:T(8,128)(2,1)} %bitcast.41) | data formatting | bytes 6291456
  206.6 1.0 convolution_convert_fusion
  207.7 0.7 copy.19
  208.4 1.7 slice.12
  210.1 4.9 %and_select_fusion = f32[6,256,256]{2,1,0:T(8,128)} fusion(bf16[3,6,256,256]{3,2,1,0:T(8,128)(2,1)S(1)} %copy-done, bf16[3,6,256,256]{3,2,1,0:T(8,128)(2,1)} %bitcast.42, bf16[3,6,256,256]{3,2,1,0:T(8,128)(2,1)} %param.6, pred[6,256]{1,0:T(8,128)(4,1)S(1)} %get-tuple-element.8, pred[6,256]{1,0:T(8,128)(4,1)S(1)} %get-tuple-element.9), kind=kOutput, calls=%fused_computation.2 | convolution fusion | flops 1209925632 | bytes 8653824 | tf_op jit(solution)/shard_map/bkil,bkml->bkim/dot_general | solution.py:41
  215.0 0.0 reduce-scatter.2.cloned.1.call-update
  215.0 1.6 constant_dynamic-slice_fusion
  216.7 32.8 %reduce-scatter.2.cloned.1.call-done = f32[6,32,256]{2,1,0:T(8,128)} async-done(((f32[6,256,256]{2,1,0:T(8,128)}), f32[6,32,256]{2,1,0:T(8,128)}) %reduce-scatter.2.cloned.1.call-update) | async-done | bytes 196624 | tf_op jit(solution)/shard_map/reduce_scatter | solution.py:66
Async XLA Ops:
  7.2 57.2 %copy-start = (bf16[3,6,256,256]{3,2,1,0:T(8,128)(2,1)S(1)}, bf16[3,6,256,256]{3,2,1,0:T(8,128)(2,1)}, u32[]{:S(2)}) copy-start(bf16[3,6,256,256]{3,2,1,0:T(8,128)(2,1)} %param.7) | copy-start | bytes 7077892
  7.2 3.4 %copy-start.2 = (s32[3,24]{1,0:T(4,128)S(1)}, s32[3,24]{1,0:T(4,128)}, u32[]{:S(2)}) copy-start(s32[3,24]{1,0:T(4,128)} %param.8) | copy-start | bytes 868
  7.2 50.1 %all-gather.3.cloned.1.call-start = ((), (), s32[]{:S(2)}) async-start(), calls=%async_computation.1 | async-start | bytes 3932160 | tf_op jit(solution)/shard_map/all_gather | solution.py:25
  10.5 120.9 %all-reduce.3.cloned.1.call-start = ((), (), s32[]{:S(2)}) async-start(), calls=%async_computation.2 | async-start | bytes 3145728 | tf_op jit(solution)/shard_map/psum | solution.py:57
  64.4 67.1 %copy-start.1 = (bf16[6,256,256]{2,1,0:T(8,128)(2,1)S(1)}, bf16[6,256,256]{2,1,0:T(8,128)(2,1)}, u32[]{:S(2)}) copy-start(bf16[6,256,256]{2,1,0:T(8,128)(2,1)} %param.5) | copy-start | bytes 2359300
  69.4 133.6 %all-gather.5.cloned.1.call-start = ((), (), s32[]{:S(2)}) async-start(), calls=%async_computation.3 | async-start | bytes 3932160 | tf_op jit(solution)/shard_map/all_gather | solution.py:25
  160.6 88.8 %reduce-scatter.2.cloned.1.call-start = ((), (), s32[]{:S(2)}) async-start(), calls=%async_computation.4 | async-start | bytes 1769472 | tf_op jit(solution)/shard_map/reduce_scatter | solution.py:66
Sparse Core Ops, SparseCore 0:
  10.7 46.5 all-gather.2
  69.5 61.8 all-reduce.2
  160.7 42.1 all-gather.4
  215.1 34.2 reduce-scatter.1
where the time goes:
time: 256 us
  waiting for transfers between devices  183 us (71%)
  blocking collectives  19 us (7%)
  between operations  15.9 us (6%)
  local copies, waits for them, and re-layouts  14.8 us (6%)
  matrix products  12 us (5%)
  other arithmetic  10.5 us (4%)
    all_gather x2, waiting for transfers between devices, fetch_blocks(): pieces = lax.all_gather(masked, 'sector', axis=0, tiled=True)  88.6 us
    psum x1, waiting for transfers between devices, body(): whole_sum = lax.psum(partial_value, 'term')  62 us
    reduce_scatter x1, waiting for transfers between devices, body(): lax.psum_scatter(second_partial, 'term', scatter_dimension=1, tiled=True)  32.8 us
    unnamed x12, local copies, waits for them, and re-layouts  12.1 us
    psum x1, blocking collectives, body(): lax.psum((jnp.sum(masked_float * whole_sum), jnp.sum(masked_float * maske...  10.4 us
    dot_general x2, matrix products, apply_operator(): jnp.einsum('bkil,bkml->bkim', half_product, right_env, preferred_element_...  9.96 us
    psum x1, blocking collectives, body(): spread = lax.psum(jnp.sum(residual * residual), 'sector')  8.58 us
    select_n x2, other arithmetic, apply_operator(): masked = jnp.where(keep, vector, jnp.zeros_like(vector))  5.17 us
  transfers between devices with their start and end apart: 4, of which 4 were waited for; matrix products, arithmetic and copies ran while one was open for 1% of the time, Pallas kernels for 0%

commit v1 on v0

--- a/solution.py
+++ b/solution.py
@@ -54,7 +54,11 @@
     total_count = lax.axis_size("sector") * wavefunction.shape[0] * width * width
     partial_value, masked = apply_operator(wavefunction, left_env, right_env, source, keep)
     masked_float = masked.astype(jnp.float32)
-    whole_sum = lax.psum(partial_value, "term")
+    whole_sum = partial_value
+    for hop in (1, 2, 4):
+        whole_sum = whole_sum + lax.ppermute(
+            whole_sum, "term", [(dev, dev ^ hop) for dev in range(8)]
+        )
     first_product = lax.dynamic_slice_in_dim(whole_sum, term_index * row_count, row_count, 1)
     margin, self_norm = lax.psum(
         (jnp.sum(masked_float * whole_sum), jnp.sum(masked_float * masked_float)), "sector"

time: 256 us -> 308 us (1.20)
  waiting for transfers between devices: 183 us -> 229 us
  starting transfers between devices: 0.34 us -> 4.33 us
    ppermute x0 -> x3, waiting for transfers between devices: none -> 106 us  [body(): lax.ppermute(whole_sum, 'term', [(dev, dev ^ hop) for dev in range(8)])]
    psum x1 -> x0, waiting for transfers between devices: 62 us -> none  [body(): whole_sum = lax.psum(partial_value, 'term')]
    ppermute x0 -> x3, starting transfers between devices: none -> 4.03 us  [body(): lax.ppermute(whole_sum, 'term', [(dev, dev ^ hop) for dev in range(8)])]
  transfers between devices with their start and end apart: 4 -> 6, of which waited for: 4 -> 6; matrix products, arithmetic and copies ran while one was open for 1% -> 1% of each run, Pallas kernels for 0% -> 0%
where the time goes in v1:
time: 308 us; the launch traced here: 307 us
  waiting for transfers between devices  229 us (74%)
  blocking collectives  19 us (6%)
  between operations  15.9 us (5%)
  local copies, waits for them, and re-layouts  14.7 us (5%)
  other arithmetic  11.9 us (4%)
  matrix products  11.9 us (4%)
  starting transfers between devices  4.33 us (1%)
    ppermute x3, waiting for transfers between devices, body(): lax.ppermute(whole_sum, 'term', [(dev, dev ^ hop) for dev in range(8)])  106 us
    all_gather x2, waiting for transfers between devices, fetch_blocks(): pieces = lax.all_gather(masked, 'sector', axis=0, tiled=True)  90.2 us
    reduce_scatter x1, waiting for transfers between devices, body(): lax.psum_scatter(second_partial, 'term', scatter_dimension=1, tiled=True)  32.8 us
    unnamed x12, local copies, waits for them, and re-layouts  12.1 us
    dot_general x2, matrix products, apply_operator(): jnp.einsum('bkil,bkml->bkim', half_product, right_env, preferred_element_...  9.89 us
    psum x1, blocking collectives, body(): lax.psum((jnp.sum(masked_float * whole_sum), jnp.sum(masked_float * maske...  9.54 us
    psum x1, blocking collectives, body(): spread = lax.psum(jnp.sum(residual * residual), 'sector')  9.48 us
  transfers between devices with their start and end apart: 6, of which 6 were waited for; matrix products, arithmetic and copies ran while one was open for 1% of the time, Pallas kernels for 0%

profile of v1, /device:TPU:0, one launch (start us, length us, event | category | flops | bytes accessed | tf_op | source)
XLA Modules:
  0.0 307.2 jit_solution(14480037930609289921)
XLA Ops:
  7.2 0.0 copy-start
  7.2 0.0 copy-start.2
  7.2 0.0 all-gather.3.cloned.1.call-start
  7.2 0.9 slice_bitcast_fusion.1
  8.1 0.1 iota_compare_fusion.3
  8.2 2.3 and_select_fusion.3
  10.5 0.0 all-gather.3.cloned.1.call-update
  10.5 0.0 all-gather.5.cloned.1.call-start
  10.6 0.0 copy-done.2
  10.6 0.1 constant_dynamic-slice_fusion.1
  10.7 0.1 eq.8
  10.8 46.5 %all-gather.3.cloned.1.call-done = bf16[24,256,256]{2,1,0:T(8,128)(2,1)} async-done(((bf16[6,256,256]{2,1,0:T(8,128)(2,1)}), bf16[24,256,256]{2,1,0:T(8,128)(2,1)}) %all-gather.3.cloned.1.call-update) | async-done | bytes 3145744 | tf_op jit(solution)/shard_map/all_gather | solution.py:25
  57.3 3.7 %copy.16 = bf16[3,8,256,256]{3,1,2,0:T(8,128)(2,1)S(1)} copy(bf16[3,8,256,256]{3,2,1,0:T(8,128)(2,1)} %bitcast.40) | data formatting | bytes 6291456
  60.9 1.0 convolution_convert_fusion.1
  62.0 0.7 copy.17
  62.7 1.6 slice.11
  64.3 0.0 copy-done
  64.3 4.9 %and_select_fusion.2 = f32[6,256,256]{2,1,0:T(8,128)} fusion(bf16[3,6,256,256]{3,2,1,0:T(8,128)(2,1)S(1)} %copy-done, bf16[3,6,256,256]{3,2,1,0:T(8,128)(2,1)} %bitcast.43, bf16[3,6,256,256]{3,2,1,0:T(8,128)(2,1)} %param.6, pred[6,256]{1,0:T(8,128)(4,1)S(1)} %get-tuple-element.9, pred[6,256]{1,0:T(8,128)(4,1)S(1)} %get-tuple-element.10), kind=kOutput, calls=%fused_computation.4 | convolution fusion | flops 1209925632 | bytes 8653824 | tf_op jit(solution)/shard_map/bkil,bkml->bkim/dot_general | solution.py:41
  69.3 0.0 collective-permute-start
  69.3 3.6 %collective-permute-done = f32[6,256,256]{2,1,0:T(8,128)S(1)} collective-permute-done((f32[6,256,256]{2,1,0:T(8,128)}, f32[6,256,256]{2,1,0:T(8,128)S(1)}, u32[]{:S(2)}, u32[]{:S(2)}) %collective-permute-start) | collective-permute-done | bytes 1572896 | tf_op jit(solution)/shard_map/ppermute | solution.py:59
  72.9 1.6 add.28
  74.5 0.0 copy-start.1
  74.5 1.6 collective-permute-start.1
  76.1 34.9 %collective-permute-done.1 = f32[6,256,256]{2,1,0:T(8,128)S(1)} collective-permute-done((f32[6,256,256]{2,1,0:T(8,128)S(1)}, f32[6,256,256]{2,1,0:T(8,128)S(1)}, u32[]{:S(2)}, u32[]{:S(2)}) %collective-permute-start.1) | collective-permute-done | bytes 1572896 | tf_op jit(solution)/shard_map/ppermute | solution.py:59
  111.0 0.2 add.29
  111.2 2.5 collective-permute-start.2
  113.7 67.8 %collective-permute-done.2 = f32[6,256,256]{2,1,0:T(8,128)S(1)} collective-permute-done((f32[6,256,256]{2,1,0:T(8,128)S(1)}, f32[6,256,256]{2,1,0:T(8,128)S(1)}, u32[]{:S(2)}, u32[]{:S(2)}) %collective-permute-start.2) | collective-permute-done | bytes 1572896 | tf_op jit(solution)/shard_map/ppermute | solution.py:59
  181.5 0.0 copy-done.1
  181.5 2.2 fusion.25
  183.7 9.5 %all-reduce = (f32[]{:T(128)}, f32[]{:T(128)}) all-reduce(f32[]{:T(128)} %get-tuple-element.3, f32[]{:T(128)} %get-tuple-element.2), channel_id=1, replica_groups=mesh['term'=8,'sector'=4] {'sector'}, use_global_device_ids=true, to_apply=%region_1.2 | all-reduce | flops 2 | bytes 16 | tf_op jit(solution)/shard_map/psum | solution.py:63
  194.6 2.6 multiply_reduce_fusion
  197.2 9.5 %psum.23 = f32[]{:T(128)} all-reduce(f32[]{:T(128)} %multiply_reduce_fusion), channel_id=1, replica_groups=mesh['term'=8,'sector'=4] {'sector'}, use_global_device_ids=true, to_apply=%region_5.6 | all-reduce | flops 1 | bytes 8 | tf_op jit(solution)/shard_map/psum | solution.py:67
  207.4 2.8 and_select_fusion.1
  210.2 0.0 all-gather.5.cloned.1.call-update
  210.3 0.2 reduce-scatter.2.cloned.1.call-start
  210.5 43.7 %all-gather.5.cloned.1.call-done = bf16[24,256,256]{2,1,0:T(8,128)(2,1)} async-done(((bf16[6,256,256]{2,1,0:T(8,128)(2,1)}), bf16[24,256,256]{2,1,0:T(8,128)(2,1)}) %all-gather.5.cloned.1.call-update) | async-done | bytes 3145744 | tf_op jit(solution)/shard_map/all_gather | solution.py:25
  254.2 3.7 %copy.18 = bf16[3,8,256,256]{3,1,2,0:T(8,128)(2,1)S(1)} copy(bf16[3,8,256,256]{3,2,1,0:T(8,128)(2,1)} %bitcast.41) | data formatting | bytes 6291456
  257.9 1.0 convolution_convert_fusion
  258.9 0.7 copy.19
  259.7 1.6 slice.12
  261.3 4.9 %and_select_fusion = f32[6,256,256]{2,1,0:T(8,128)} fusion(bf16[3,6,256,256]{3,2,1,0:T(8,128)(2,1)S(1)} %copy-done, bf16[3,6,256,256]{3,2,1,0:T(8,128)(2,1)} %bitcast.42, bf16[3,6,256,256]{3,2,1,0:T(8,128)(2,1)} %param.6, pred[6,256]{1,0:T(8,128)(4,1)S(1)} %get-tuple-element.9, pred[6,256]{1,0:T(8,128)(4,1)S(1)} %get-tuple-element.10), kind=kOutput, calls=%fused_computation.2 | convolution fusion | flops 1209925632 | bytes 8653824 | tf_op jit(solution)/shard_map/bkil,bkml->bkim/dot_general | solution.py:41
  266.3 0.0 reduce-scatter.2.cloned.1.call-update
  266.3 1.6 constant_dynamic-slice_fusion
  267.9 32.8 %reduce-scatter.2.cloned.1.call-done = f32[6,32,256]{2,1,0:T(8,128)} async-done(((f32[6,256,256]{2,1,0:T(8,128)}), f32[6,32,256]{2,1,0:T(8,128)}) %reduce-scatter.2.cloned.1.call-update) | async-done | bytes 196624 | tf_op jit(solution)/shard_map/reduce_scatter | solution.py:70
Async XLA Ops:
  7.2 57.2 %copy-start = (bf16[3,6,256,256]{3,2,1,0:T(8,128)(2,1)S(1)}, bf16[3,6,256,256]{3,2,1,0:T(8,128)(2,1)}, u32[]{:S(2)}) copy-start(bf16[3,6,256,256]{3,2,1,0:T(8,128)(2,1)} %param.7) | copy-start | bytes 7077892
  7.2 3.4 %copy-start.2 = (s32[3,24]{1,0:T(4,128)S(1)}, s32[3,24]{1,0:T(4,128)}, u32[]{:S(2)}) copy-start(s32[3,24]{1,0:T(4,128)} %param.8) | copy-start | bytes 868
  7.2 50.1 %all-gather.3.cloned.1.call-start = ((), (), s32[]{:S(2)}) async-start(), calls=%async_computation.1 | async-start | bytes 3932160 | tf_op jit(solution)/shard_map/all_gather | solution.py:25
  10.5 243.7 %all-gather.5.cloned.1.call-start = ((), (), s32[]{:S(2)}) async-start(), calls=%async_computation.2 | async-start | bytes 3932160 | tf_op jit(solution)/shard_map/all_gather | solution.py:25
  69.3 3.6 %collective-permute-start = (f32[6,256,256]{2,1,0:T(8,128)}, f32[6,256,256]{2,1,0:T(8,128)S(1)}, u32[]{:S(2)}, u32[]{:S(2)}) collective-permute-start(f32[6,256,256]{2,1,0:T(8,128)} %and_select_fusion.2), channel_id=1, source_target_pairs={{0,4},{4,0},{8,12},{12,8},{16,20},{20,16},{24,28},{28,24},{1,5},{5... | collective-permute-start | bytes 4718600 | tf_op jit(solution)/shard_map/ppermute | solution.py:59
  74.5 107.0 %copy-start.1 = (bf16[6,256,256]{2,1,0:T(8,128)(2,1)S(1)}, bf16[6,256,256]{2,1,0:T(8,128)(2,1)}, u32[]{:S(2)}) copy-start(bf16[6,256,256]{2,1,0:T(8,128)(2,1)} %param.5) | copy-start | bytes 2359300
  74.5 36.5 %collective-permute-start.1 = (f32[6,256,256]{2,1,0:T(8,128)S(1)}, f32[6,256,256]{2,1,0:T(8,128)S(1)}, u32[]{:S(2)}, u32[]{:S(2)}) collective-permute-start(f32[6,256,256]{2,1,0:T(8,128)S(1)} %add.28), channel_id=1, source_target_pairs={{0,8},{4,12},{8,0},{12,4},{16,24},{20,28},{24,16},{28,20},{1,9},{5... | collective-permute-start | bytes 4718600 | tf_op jit(solution)/shard_map/ppermute | solution.py:59
  111.2 70.3 %collective-permute-start.2 = (f32[6,256,256]{2,1,0:T(8,128)S(1)}, f32[6,256,256]{2,1,0:T(8,128)S(1)}, u32[]{:S(2)}, u32[]{:S(2)}) collective-permute-start(f32[6,256,256]{2,1,0:T(8,128)S(1)} %add.29), channel_id=1, source_target_pairs={{0,16},{4,20},{8,24},{12,28},{16,0},{20,4},{24,8},{28,12},{1,17},{... | collective-permute-start | bytes 4718600 | tf_op jit(solution)/shard_map/ppermute | solution.py:59
  210.3 90.4 %reduce-scatter.2.cloned.1.call-start = ((), (), s32[]{:S(2)}) async-start(), calls=%async_computation.3 | async-start | bytes 1769472 | tf_op jit(solution)/shard_map/reduce_scatter | solution.py:70
Sparse Core Ops, SparseCore 0:
  10.6 46.5 all-gather.2
  210.4 43.8 all-gather.4
  266.4 34.2 reduce-scatter.1
